TPU v7x, 512 devices: a 4x2x32 block of a 4x8x32 slice. The times are simulated.
512 devices in a mesh: grp: 2 (over y), wide: 128 (over x, z), narrow: 2 (over core).
Axes of the slice: x: 4, y: 2, z: 32, core: 2. Of those that a mesh axis runs over, the one named last changes fastest.
The devices are a block of a 4x8x32 slice.
Arguments:
- cache: bfloat16 [256, 768, 576], P('grp', ('wide', 'narrow')), parts along dimension 0, may hold values from -4 to 4
- lengths: int32 [256], P('grp'), parts along dimension 0, may hold values from 1 to 767, 32768 in all
- slots: int32 [256], P('grp'), parts along dimension 0, may hold values from 0 to 127, each once
- query: bfloat16 [256, 1, 64, 576], P(('grp', 'wide'), None, 'narrow'), parts along dimension 0, may hold values from -200 to 200
Outputs:
- attended: bfloat16 [256, 1, 64, 512], P(('grp', 'wide'), None, 'narrow'), parts along dimension 0
There are 2 independent parts, one for each index of `grp`. A program takes and returns all parts, laid end to end along the dimension named above; each array names one. Nothing has to cross between parts.
Inputs may be any that keep to these rules, and one draw needn't show every extreme that they name: `lengths`: each request has at most 767 cached positions, and some request has exactly that many in every draw; its 1 new tokens' entries follow its cached positions. `slots`: A permutation: every slot holds one request.
All inputs are finite; a program needn't handle non-finite values.
Results may differ from a plain program's by a relative error of at most 0.013.
Values may be sent and summed in bfloat16 or wider, within the bound.
No kernel may reach another device: no remote copies, remote signals or barrier semaphores. Data moves between devices by JAX's collectives and lax.ppermute only.
A program may use at most 64 MiB of HBM per device.

v0:
```python
import jax
import jax.numpy as jnp
from jax import lax
from jax.sharding import PartitionSpec as P

LATENT_WIDTH = 512


score_scale = 0.0721687836
floor_value = -1e30


def key_positions(row_index, shard_rows, narrow_base, wide_count, narrow_count):
    group_rows = wide_count * shard_rows
    narrow_part = narrow_base + row_index // group_rows
    within = row_index % group_rows
    source = within // shard_rows
    offset = within % shard_rows
    return (source * narrow_count + narrow_part) * shard_rows + offset


def absorb(running, query_rows, cache_key_rows, places, key_limit):
    running_max, weight_sum, latent_total = running
    scores = (
        lax.dot_general(
            query_rows, cache_key_rows, (((1,), (1,)), ((), ())), preferred_element_type=jnp.float32
        )
        * score_scale
    )
    visible = places[None, :] < key_limit[:, None]
    scores = jnp.where(visible, scores, floor_value)
    newest = jnp.maximum(running_max, jnp.max(scores, axis=1))
    softmax_weights = jnp.where(visible, jnp.exp(scores - newest[:, None]), 0.0)
    weight_sum = jnp.sum(softmax_weights, axis=1)
    latent_total = jnp.dot(
        softmax_weights.astype(jnp.bfloat16),
        cache_key_rows[:, :LATENT_WIDTH],
        preferred_element_type=jnp.float32,
    )
    return (newest, weight_sum, latent_total)


def shards(cache, lengths, slots, query):
    wide_count = lax.axis_size("wide")
    narrow_count = lax.axis_size("narrow")
    wide_index = lax.axis_index("wide")
    request_count = slots.shape[0]
    indices = jnp.arange(request_count, dtype=jnp.int32)
    owner = jnp.sum(jnp.where(slots[None, :] == indices[:, None], indices[None, :], 0), axis=1)
    ordered = jnp.take(cache, owner, axis=0)
    shard_rows = cache.shape[1]
    channels = cache.shape[2]
    received = lax.all_to_all(ordered, "wide", split_axis=0, concat_axis=1, tiled=True)
    received = received.reshape(wide_count * shard_rows, channels)
    own_length = lengths[owner[wide_index]]
    forward_steps = query.shape[1]
    head_count = query.shape[2]
    valid_row_count = forward_steps * head_count
    query_rows = query.reshape(valid_row_count, channels)
    key_limit = own_length + 1 + jnp.arange(valid_row_count, dtype=jnp.int32) // head_count
    start_state = (
        jnp.full((valid_row_count,), floor_value, jnp.float32),
        jnp.zeros((valid_row_count,), jnp.float32),
        jnp.zeros((valid_row_count, LATENT_WIDTH), jnp.float32),
    )
    block_keys = lax.all_gather(received, "narrow", axis=0, tiled=True)
    row_index = jnp.arange(block_keys.shape[0], dtype=jnp.int32)
    places = key_positions(row_index, shard_rows, 0, wide_count, narrow_count)
    running_max, weight_sum, latent_total = absorb(
        start_state, query_rows, block_keys, places, key_limit
    )
    attention_output = latent_total / weight_sum[:, None]
    return attention_output.reshape(1, forward_steps, -1, LATENT_WIDTH).astype(jnp.bfloat16)


def solution(mesh):
    return jax.shard_map(
        shards,
        mesh=mesh,
        in_specs=(
            P("grp", ("wide", "narrow"), None),
            P("grp"),
            P("grp"),
            P(("grp", "wide"), None, "narrow", None),
        ),
        out_specs=P(("grp", "wide"), None, "narrow", None),
        check_vma=False,
    )
```

profile of v0, /device:TPU:33, one launch (start us, length us, event | category | flops | bytes accessed | tf_op | source)
XLA Modules:
  0.0 136.7 jit_solution(326996921968142968)
XLA Ops:
  0.0 0.0 copy-start
  0.0 0.8 select_reduce_fusion
  0.8 1.6 %copy.6 = bf16[128,3,576]{2,1,0:T(4,128)(2,1)S(1)} copy(bf16[128,3,576]{0,2,1:T(8,128)(2,1)} %param.4) | data formatting | bytes 884736 | tf_op args[0]
  2.4 1.2 gather_fusion
  3.6 1.2 broadcast_select_fusion
  4.8 53.7 %all-to-all-start = ((bf16[128,3,576]{2,1,0:T(4,128)(2,1)}), bf16[128,3,576]{2,1,0:T(4,128)(2,1)S(1)}, u32[]{:S(2)}, u32[]{:S(2)}) async-start(bf16[128,3,576]{2,1,0:T(4,128)(2,1)} %broadcast_select_fusion), calls=%async_computation | async-start | bytes 1310720 | tf_op jit(solution)/shard_map/all_to_all | solution.py:53
  58.5 0.6 dynamic_slice.6
  60.4 0.0 copy-start.1
  61.1 0.0 copy-done.1
  61.1 0.6 dynamic_slice.7
  62.4 66.6 %all-to-all-done = bf16[128,3,576]{2,1,0:T(4,128)(2,1)S(1)} async-done(((bf16[128,3,576]{2,1,0:T(4,128)(2,1)}), bf16[128,3,576]{2,1,0:T(4,128)(2,1)S(1)}, u32[]{:S(2)}, u32[]{:S(2)}) %all-to-all-start) | async-done | bytes 442400 | tf_op jit(solution)/shard_map/all_to_all | solution.py:53
  129.0 0.4 reshape.84
  129.4 5.6 %all_gather.3 = bf16[768,576]{1,0:T(8,128)(2,1)S(1)} all-gather(bf16[384,576]{1,0:T(8,128)(2,1)S(1)} %reshape.84), channel_id=1, replica_groups=mesh['grp'=2,'wide'=128,'narrow'=2] {'narrow'}, dimensions={0}, use_global_device_ids=true | all-gather | bytes 1327104 | tf_op jit(solution)/shard_map/all_gather | solution.py:66
  135.0 0.0 copy-done
  135.1 0.5 fusion.35
  135.6 0.2 fusion.5
  135.8 0.9 fusion.3
  (6 shorter events, 0.1 us)
Async XLA Ops:
  0.0 135.1 %copy-start = (bf16[1,1,32,576]{3,2,1,0:T(8,128)(2,1)S(1)}, bf16[1,1,32,576]{3,2,1,0:T(8,128)(2,1)}, u32[]{:S(2)}) copy-start(bf16[1,1,32,576]{3,2,1,0:T(8,128)(2,1)} %param.7) | copy-start | bytes 110596
  4.8 124.2 %all-to-all-start = ((bf16[128,3,576]{2,1,0:T(4,128)(2,1)}), bf16[128,3,576]{2,1,0:T(4,128)(2,1)S(1)}, u32[]{:S(2)}, u32[]{:S(2)}) async-start(bf16[128,3,576]{2,1,0:T(4,128)(2,1)} %broadcast_select_fusion), calls=%async_computation | async-start | bytes 1310720 | tf_op jit(solution)/shard_map/all_to_all | solution.py:53
  60.4 0.7 copy-start.1
where the time goes:
time: 137 us
  waiting for transfers between devices  66.6 us (49%)
  starting transfers between devices  53.7 us (39%)
  blocking collectives  5.62 us (4%)
  local copies, waits for them, and re-layouts  4.37 us (3%)
  between operations  2.7 us (2%)
  other arithmetic  2.25 us (2%)
  matrix products  1.43 us (1%)
    all_to_all x1, waiting for transfers between devices, shards(): lax.all_to_all(ordered, 'wide', split_axis=0, concat_axis=1, tiled=True)  66.6 us
    all_to_all x1, starting transfers between devices, shards(): lax.all_to_all(ordered, 'wide', split_axis=0, concat_axis=1, tiled=True)  53.7 us
    all_gather x1, blocking collectives, shards(): block_keys = lax.all_gather(received, 'narrow', axis=0, tiled=True)  5.62 us
  transfers between devices with their start and end apart: 1, of which 1 were waited for; matrix products, arithmetic and copies ran while one was open for 1% of the time, Pallas kernels for 0%

commit v1 on v0

v1 whole, which is shorter than its diff:
```python
import jax
import jax.numpy as jnp
from jax import lax
from jax.experimental import pallas as pl
from jax.experimental.pallas import tpu as pltpu
from jax.sharding import PartitionSpec as P

LATENT_WIDTH = 512
COLUMNS = 4

score_scale = 0.0721687836
floor_value = -1e30

NT = (((1,), (1,)), ((), ()))
NN = (((1,), (0,)), ((), ()))


def pack_kernel(rows, slots_ref, cache_ref, packed_ref):
    count = slots_ref.shape[1]
    rotary = cache_ref.shape[1] - LATENT_WIDTH
    half, half_rotary = LATENT_WIDTH // 2, rotary // 2
    parts = []
    for h in range(2):
        parts.append(
            jnp.concatenate(
                [
                    cache_ref[h, :LATENT_WIDTH, :],
                    cache_ref[2, half * h : half * (h + 1), :],
                    cache_ref[h, LATENT_WIDTH:, :],
                    cache_ref[2, LATENT_WIDTH + half_rotary * h : LATENT_WIDTH + half_rotary * (h + 1), :],
                    jnp.zeros((half_rotary, count), cache_ref.dtype),
                ],
                axis=0,
            )
        )
    table = jnp.concatenate(parts, axis=1)
    slots = jnp.concatenate([slots_ref[...]] * 2, axis=1)
    row = lax.broadcasted_iota(jnp.int32, (2 * count, 1), 0)
    place = row // 2
    target = (place % COLUMNS) * rows + place // COLUMNS
    side = lax.broadcasted_iota(jnp.int32, (1, 2 * count), 1) // count
    chosen = (slots == target) & (side == row % 2)
    select = jnp.where(chosen, 1.0, 0.0).astype(cache_ref.dtype)
    packed_ref[...] = lax.dot_general(select, table, NT, preferred_element_type=jnp.float32).astype(
        packed_ref.dtype
    )


def attend_kernel(rows, me_ref, slots_ref, lengths_ref, query_ref, keys_ref, out_ref):
    heads = out_ref.shape[0]
    width = keys_ref.shape[0]
    half = LATENT_WIDTH // 2
    limit = 1 + jnp.sum(jnp.where(slots_ref[...] == me_ref[0], lengths_ref[...], 0), axis=1, keepdims=True)
    scores = lax.dot_general(query_ref[...], keys_ref[...], NT, preferred_element_type=jnp.float32) * score_scale
    lane = lax.broadcasted_iota(jnp.int32, (1, width), 1)
    side = lane % 2
    place = (lane // 2) % (width // 4)
    source = (place % COLUMNS) * rows + place // COLUMNS
    first = (source * 2 + lane // (width // 2)) * 3
    whole = scores[:heads]
    part = jnp.where(side == 0, scores[heads : 2 * heads], scores[2 * heads :])
    joined = part + jnp.where(side == 0, pltpu.roll(part, width - 1, 1), pltpu.roll(part, 1, 1))
    whole = jnp.where(first + side < limit, whole, floor_value)
    joined = jnp.where(first + 2 < limit, joined, floor_value)
    highest = jnp.max(jnp.maximum(whole, joined), axis=1, keepdims=True)
    whole = jnp.exp(whole - highest)
    joined = jnp.exp(joined - highest)
    even = jnp.where(side == 0, joined, 0.0)
    odd = joined - even
    weight_sum = jnp.sum(whole + even, axis=1, keepdims=True)
    latent = lax.dot_general(
        whole.astype(keys_ref.dtype), keys_ref[:, :LATENT_WIDTH], NN, preferred_element_type=jnp.float32
    )
    halves = lax.dot_general(
        jnp.concatenate([even, odd], axis=0).astype(keys_ref.dtype),
        keys_ref[:, LATENT_WIDTH : LATENT_WIDTH + half],
        NN,
        preferred_element_type=jnp.float32,
    )
    latent = latent + jnp.concatenate([halves[:heads], halves[heads:]], axis=1)
    out_ref[...] = (latent / weight_sum).astype(out_ref.dtype)


def shards(cache, lengths, slots, query):
    wide_count = lax.axis_size("wide")
    rows = wide_count // COLUMNS
    count = slots.shape[0]
    channels = cache.shape[2]
    rotary = channels - LATENT_WIDTH
    half, half_rotary = LATENT_WIDTH // 2, rotary // 2
    heads = query.shape[2]
    packed_width = LATENT_WIDTH + half + 2 * rotary
    slot_row = slots.reshape(1, count)
    length_row = lengths.reshape(1, count)
    packed = pl.pallas_call(
        lambda *refs: pack_kernel(rows, *refs),
        out_shape=jax.ShapeDtypeStruct((2 * count, packed_width), cache.dtype),
        name="pack",
    )(slot_row, jnp.transpose(cache, (1, 2, 0)))
    order = [x * rows + z for z in range(rows) for x in range(COLUMNS)]
    received = lax.all_to_all(
        packed.reshape(count, 2, packed_width), "wide", 0, 0, tiled=True, axis_index_groups=[order]
    )
    keys = lax.all_gather(received.reshape(2 * count, packed_width), "narrow", axis=0, tiled=True)
    q = query.reshape(heads, channels)
    latent, turned = q[:, :LATENT_WIDTH], q[:, LATENT_WIDTH:]

    def blank(n):
        return jnp.zeros((heads, n), q.dtype)

    stacked = [jnp.concatenate([latent, blank(half), turned, blank(rotary)], axis=1)]
    for h in range(2):
        stacked.append(
            jnp.concatenate(
                [
                    blank(LATENT_WIDTH),
                    latent[:, half * h : half * (h + 1)],
                    blank(rotary),
                    turned[:, half_rotary * h : half_rotary * (h + 1)],
                    blank(half_rotary),
                ],
                axis=1,
            )
        )
    queries = jnp.concatenate(stacked, axis=0)
    me = lax.axis_index("wide").astype(jnp.int32).reshape(1)
    vmem = pl.BlockSpec(memory_space=pltpu.VMEM)
    attended = pl.pallas_call(
        lambda *refs: attend_kernel(rows, *refs),
        out_shape=jax.ShapeDtypeStruct((heads, LATENT_WIDTH), jnp.bfloat16),
        in_specs=[pl.BlockSpec(memory_space=pltpu.SMEM), vmem, vmem, vmem, vmem],
        out_specs=vmem,
        name="attend",
    )(me, slot_row, length_row, queries, keys)
    return attended.reshape(1, 1, heads, LATENT_WIDTH)


def solution(mesh):
    return jax.shard_map(
        shards,
        mesh=mesh,
        in_specs=(
            P("grp", ("wide", "narrow"), None),
            P("grp"),
            P("grp"),
            P(("grp", "wide"), None, "narrow", None),
        ),
        out_specs=P(("grp", "wide"), None, "narrow", None),
        check_vma=False,
    )
```

time: 137 us -> 118 us (0.86)
  the two profiles are of different devices: /device:TPU:33 before, /device:TPU:39 now
where the time goes in v1:
time: 118 us; the launch traced here: 117 us
  waiting for transfers between devices  52.4 us (44%)
  starting transfers between devices  50.2 us (43%)
  blocking collectives  6.46 us (5%)
  Pallas kernels  4.95 us (4%)
  local copies, waits for them, and re-layouts  2.43 us (2%)
    all_to_all x1, waiting for transfers between devices, shards(): lax.all_to_all(packed.reshape(count, 2, packed_width), 'wide', 0, 0, tile...  52.4 us
    all_to_all x1, starting transfers between devices, shards(): lax.all_to_all(packed.reshape(count, 2, packed_width), 'wide', 0, 0, tile...  50.2 us
    all_gather x1, blocking collectives, shards(): lax.all_gather(received.reshape(2 * count, packed_width), 'narrow', axis=...  6.46 us
    pallas_call x1, Pallas kernels, shards(): pl.pallas_call(lambda *refs: attend_kernel(rows, *refs), out_shape=jax.Sh...  2.81 us
  transfers between devices with their start and end apart: 1, of which 1 were waited for; matrix products, arithmetic and copies ran while one was open for 1% of the time, Pallas kernels for 0%

profile of v1, /device:TPU:39, one launch (start us, length us, event | category | flops | bytes accessed | tf_op | source)
XLA Modules:
  0.0 117.3 jit_solution(5370834187608061596)
XLA Ops:
  0.0 2.1 %pack.1 = bf16[256,896]{1,0:T(8,128)(2,1)} custom-call(s32[1,128]{1,0:T(1,128)} %bitcast.11, bf16[3,576,128]{2,1,0:T(8,128)(2,1)} %bitcast.6), custom_call_target="tpu_custom_call" | custom-call | tf_op jit(solution)/shard_map/pack/pallas_call | solution.py:95
  2.1 2.0 %reshape.25 = bf16[128,2,896]{2,1,0:T(2,128)(2,1)} reshape(bf16[256,896]{1,0:T(8,128)(2,1)} %pack.1) | data formatting | bytes 917504 | tf_op jit(solution)/shard_map/reshape | solution.py:102
  4.1 0.0 copy-start
  4.1 50.2 %all-to-all-start = ((bf16[128,2,896]{2,1,0:T(2,128)(2,1)}), bf16[128,2,896]{2,1,0:T(2,128)(2,1)S(1)}, u32[]{:S(2)}, u32[]{:S(2)}) async-start(bf16[128,2,896]{2,1,0:T(2,128)(2,1)} %reshape.25), calls=%async_computation | async-start | bytes 917504 | tf_op jit(solution)/shard_map/all_to_all | solution.py:101
  54.3 0.0 copy-done
  54.4 0.1 fusion
  54.5 0.1 concatenate.13
  54.6 0.1 concatenate.14
  54.7 0.7 pad_maximum_fusion.refs_3_
  55.4 52.4 %all-to-all-done = bf16[128,2,896]{2,1,0:T(2,128)(2,1)S(1)} async-done(((bf16[128,2,896]{2,1,0:T(2,128)(2,1)}), bf16[128,2,896]{2,1,0:T(2,128)(2,1)S(1)}, u32[]{:S(2)}, u32[]{:S(2)}) %all-to-all-start) | async-done | bytes 458784 | tf_op jit(solution)/shard_map/all_to_all | solution.py:101
  107.8 0.2 reshape.26
  108.0 6.5 %all_gather.3.refs_4_ = bf16[512,896]{1,0:T(8,128)(2,1)} all-gather(bf16[256,896]{1,0:T(8,128)(2,1)S(1)} %reshape.26), channel_id=1, replica_groups=mesh['grp'=2,'wide'=128,'narrow'=2] {'narrow'}, dimensions={0}, use_global_device_ids=true | all-gather | bytes 1376256 | tf_op jit(solution)/shard_map/all_gather | solution.py:104
  114.5 2.8 %attend.1 = bf16[32,512]{1,0:T(8,128)(2,1)} custom-call(s32[1]{0:T(128)} %bitcast.refs_0_, s32[1,128]{1,0:T(1,128)} %bitcast.12, s32[1,128]{1,0:T(1,128)} %bitcast.13, bf16[96,896]{1,0:T(8,128)(2,1)} %pad_maximum_fusion.refs_3_, bf16[512,896]{1,0:T(8,128)(2,1)} %all_gather.3.refs_4_), custom_call_target="tpu_custom_call" | custom-call | tf_op jit(solution)/shard_map/attend/pallas_call | solution.py:128
  (7 shorter events, 0.0 us)
Async XLA Ops:
  4.1 50.3 %copy-start = (bf16[1,1,32,576]{3,2,1,0:T(8,128)(2,1)S(1)}, bf16[1,1,32,576]{3,2,1,0:T(8,128)(2,1)}, u32[]{:S(2)}) copy-start(bf16[1,1,32,576]{3,2,1,0:T(8,128)(2,1)} %param.7) | copy-start | bytes 110596
  4.1 103.7 %all-to-all-start = ((bf16[128,2,896]{2,1,0:T(2,128)(2,1)}), bf16[128,2,896]{2,1,0:T(2,128)(2,1)S(1)}, u32[]{:S(2)}, u32[]{:S(2)}) async-start(bf16[128,2,896]{2,1,0:T(2,128)(2,1)} %reshape.25), calls=%async_computation | async-start | bytes 917504 | tf_op jit(solution)/shard_map/all_to_all | solution.py:101

commit v2 on v1

--- a/solution.py
+++ b/solution.py
@@ -7,12 +7,20 @@
 
 LATENT_WIDTH = 512
 COLUMNS = 4
+VMEM_BYTES = 8 << 20
 
 score_scale = 0.0721687836
 floor_value = -1e30
 
 NT = (((1,), (1,)), ((), ()))
 NN = (((1,), (0,)), ((), ()))
+
+
+def partner(place, rows):
+    step, row = place // COLUMNS, 0
+    for b in range(rows.bit_length() - 1):
+        row = row * 2 + (step >> b) % 2
+    return (place % COLUMNS) * rows + row
 
 
 def pack_kernel(rows, slots_ref, cache_ref, packed_ref):
@@ -37,25 +45,42 @@
     slots = jnp.concatenate([slots_ref[...]] * 2, axis=1)
     row = lax.broadcasted_iota(jnp.int32, (2 * count, 1), 0)
     place = row // 2
-    target = (place % COLUMNS) * rows + place // COLUMNS
+    target = partner(place, rows)
     side = lax.broadcasted_iota(jnp.int32, (1, 2 * count), 1) // count
     chosen = (slots == target) & (side == row % 2)
     select = jnp.where(chosen, 1.0, 0.0).astype(cache_ref.dtype)
-    packed_ref[...] = lax.dot_general(select, table, NT, preferred_element_type=jnp.float32).astype(
-        packed_ref.dtype
-    )
+    packed = lax.dot_general(select, table, NT, preferred_element_type=jnp.float32).astype(packed_ref.dtype)
+    packed_ref[...] = packed.reshape(packed_ref.shape)
 
 
-def attend_kernel(rows, me_ref, slots_ref, lengths_ref, query_ref, keys_ref, out_ref):
+def query_kernel(me_ref, slots_ref, lengths_ref, query_ref, stacked_ref, limit_ref):
+    heads = query_ref.shape[0]
+    rotary = query_ref.shape[1] - LATENT_WIDTH
+    half, half_rotary = LATENT_WIDTH // 2, rotary // 2
+    stacked_ref[...] = jnp.zeros_like(stacked_ref)
+    tail = LATENT_WIDTH + half
+    stacked_ref[:heads, :LATENT_WIDTH] = query_ref[:, :LATENT_WIDTH]
+    stacked_ref[:heads, tail : tail + rotary] = query_ref[:, LATENT_WIDTH:]
+    for h in range(2):
+        rows = pl.ds(heads * (h + 1), heads)
+        stacked_ref[rows, LATENT_WIDTH:tail] = query_ref[:, half * h : half * (h + 1)]
+        stacked_ref[rows, tail + rotary : tail + rotary + half_rotary] = query_ref[
+            :, LATENT_WIDTH + half_rotary * h : LATENT_WIDTH + half_rotary * (h + 1)
+        ]
+    own = jnp.where(slots_ref[...] == me_ref[0], lengths_ref[...], 0)
+    limit_ref[...] = jnp.broadcast_to(1 + jnp.sum(own, axis=1, keepdims=True), limit_ref.shape)
+
+
+def attend_kernel(rows, limit_ref, query_ref, keys_ref, out_ref):
     heads = out_ref.shape[0]
     width = keys_ref.shape[0]
     half = LATENT_WIDTH // 2
-    limit = 1 + jnp.sum(jnp.where(slots_ref[...] == me_ref[0], lengths_ref[...], 0), axis=1, keepdims=True)
+    limit = limit_ref[:, :1]
     scores = lax.dot_general(query_ref[...], keys_ref[...], NT, preferred_element_type=jnp.float32) * score_scale
     lane = lax.broadcasted_iota(jnp.int32, (1, width), 1)
     side = lane % 2
     place = (lane // 2) % (width // 4)
-    source = (place % COLUMNS) * rows + place // COLUMNS
+    source = partner(place, rows)
     first = (source * 2 + lane // (width // 2)) * 3
     whole = scores[:heads]
     part = jnp.where(side == 0, scores[heads : 2 * heads], scores[2 * heads :])
@@ -87,51 +112,41 @@
     count = slots.shape[0]
     channels = cache.shape[2]
     rotary = channels - LATENT_WIDTH
-    half, half_rotary = LATENT_WIDTH // 2, rotary // 2
     heads = query.shape[2]
-    packed_width = LATENT_WIDTH + half + 2 * rotary
+    packed_width = LATENT_WIDTH + LATENT_WIDTH // 2 + 2 * rotary
     slot_row = slots.reshape(1, count)
-    length_row = lengths.reshape(1, count)
     packed = pl.pallas_call(
         lambda *refs: pack_kernel(rows, *refs),
-        out_shape=jax.ShapeDtypeStruct((2 * count, packed_width), cache.dtype),
+        out_shape=jax.ShapeDtypeStruct((count, 2, packed_width), cache.dtype),
         name="pack",
     )(slot_row, jnp.transpose(cache, (1, 2, 0)))
-    order = [x * rows + z for z in range(rows) for x in range(COLUMNS)]
+    order = [partner(place, rows) for place in range(wide_count)]
     received = lax.all_to_all(
-        packed.reshape(count, 2, packed_width), "wide", 0, 0, tiled=True, axis_index_groups=[order]
+        packed, "wide", 0, 0, tiled=True, axis_index_groups=[order]
     )
     keys = lax.all_gather(received.reshape(2 * count, packed_width), "narrow", axis=0, tiled=True)
-    q = query.reshape(heads, channels)
-    latent, turned = q[:, :LATENT_WIDTH], q[:, LATENT_WIDTH:]
-
-    def blank(n):
-        return jnp.zeros((heads, n), q.dtype)
-
-    stacked = [jnp.concatenate([latent, blank(half), turned, blank(rotary)], axis=1)]
-    for h in range(2):
-        stacked.append(
-            jnp.concatenate(
-                [
-                    blank(LATENT_WIDTH),
-                    latent[:, half * h : half * (h + 1)],
-                    blank(rotary),
-                    turned[:, half_rotary * h : half_rotary * (h + 1)],
-                    blank(half_rotary),
-                ],
-                axis=1,
-            )
-        )
-    queries = jnp.concatenate(stacked, axis=0)
     me = lax.axis_index("wide").astype(jnp.int32).reshape(1)
     vmem = pl.BlockSpec(memory_space=pltpu.VMEM)
+    stacked, limit = pl.pallas_call(
+        query_kernel,
+        out_shape=(
+            jax.ShapeDtypeStruct((3 * heads, packed_width), query.dtype),
+            jax.ShapeDtypeStruct((1, count), jnp.int32),
+        ),
+        in_specs=[pl.BlockSpec(memory_space=pltpu.SMEM), vmem, vmem, vmem],
+        out_specs=(vmem, vmem),
+        compiler_params=pltpu.CompilerParams(vmem_limit_bytes=VMEM_BYTES),
+        cost_estimate=pl.CostEstimate(flops=1 << 22, bytes_accessed=1 << 18, transcendentals=0),
+        name="stack",
+    )(me, slot_row, lengths.reshape(1, count), query.reshape(heads, channels))
     attended = pl.pallas_call(
         lambda *refs: attend_kernel(rows, *refs),
         out_shape=jax.ShapeDtypeStruct((heads, LATENT_WIDTH), jnp.bfloat16),
-        in_specs=[pl.BlockSpec(memory_space=pltpu.SMEM), vmem, vmem, vmem, vmem],
+        in_specs=[vmem, vmem, vmem],
         out_specs=vmem,
+        compiler_params=pltpu.CompilerParams(vmem_limit_bytes=VMEM_BYTES),
         name="attend",
-    )(me, slot_row, length_row, queries, keys)
+    )(limit, stacked, keys)
     return attended.reshape(1, 1, heads, LATENT_WIDTH)
 
 

time: 118 us -> 110 us (0.932)
  the two profiles are of different devices: /device:TPU:39 before, /device:TPU:33 now
where the time goes in v2:
time: 110 us; the launch traced here: 109 us
  starting transfers between devices  53.8 us (49%)
  waiting for transfers between devices  45.8 us (42%)
  blocking collectives  4.49 us (4%)
  Pallas kernels  3.95 us (4%)
    all_to_all x1, starting transfers between devices, shards(): lax.all_to_all(packed, 'wide', 0, 0, tiled=True, axis_index_groups=[order])  53.8 us
    all_to_all x1, waiting for transfers between devices, shards(): lax.all_to_all(packed, 'wide', 0, 0, tiled=True, axis_index_groups=[order])  45.8 us
    all_gather x1, blocking collectives, shards(): lax.all_gather(received.reshape(2 * count, packed_width), 'narrow', axis=...  4.49 us
    pallas_call x1, Pallas kernels, shards(): pl.pallas_call(lambda *refs: pack_kernel(rows, *refs), out_shape=jax.Shap...  2.35 us
  transfers between devices with their start and end apart: 1, of which 1 were waited for; matrix products, arithmetic and copies ran while one was open for 0% of the time, Pallas kernels for 0%

profile of v2, /device:TPU:33, one launch (start us, length us, event | category | flops | bytes accessed | tf_op | source)
XLA Modules:
  0.0 109.0 jit_solution(7284213539423484208)
XLA Ops:
  0.0 2.4 %pack.1 = bf16[128,2,896]{2,1,0:T(2,128)(2,1)} custom-call(s32[1,128]{1,0:T(1,128)} %bitcast.7, bf16[3,576,128]{2,1,0:T(8,128)(2,1)} %bitcast.10), custom_call_target="tpu_custom_call" | custom-call | tf_op jit(solution)/shard_map/pack/pallas_call | solution.py:118
  2.4 0.0 copy-start
  2.4 53.8 %all-to-all-start = ((bf16[128,2,896]{2,1,0:T(2,128)(2,1)}), bf16[128,2,896]{2,1,0:T(2,128)(2,1)S(1)}, u32[]{:S(2)}, u32[]{:S(2)}) async-start(bf16[128,2,896]{2,1,0:T(2,128)(2,1)} %pack.1), calls=%async_computation | async-start | bytes 917504 | tf_op jit(solution)/shard_map/all_to_all | solution.py:124
  56.2 0.0 copy-start.1
  56.2 0.0 copy-start.2
  56.2 0.0 copy-done
  56.2 0.6 copy-done.1
  56.9 0.0 copy-done.2
  56.9 0.1 stack.1
  57.0 45.8 %all-to-all-done = bf16[128,2,896]{2,1,0:T(2,128)(2,1)S(1)} async-done(((bf16[128,2,896]{2,1,0:T(2,128)(2,1)}), bf16[128,2,896]{2,1,0:T(2,128)(2,1)S(1)}, u32[]{:S(2)}, u32[]{:S(2)}) %all-to-all-start) | async-done | bytes 458784 | tf_op jit(solution)/shard_map/all_to_all | solution.py:124
  102.8 0.2 reshape.22
  103.0 4.5 %all_gather.3.refs_2_ = bf16[512,896]{1,0:T(8,128)(2,1)S(1)} all-gather(bf16[256,896]{1,0:T(8,128)(2,1)S(1)} %reshape.22), channel_id=1, replica_groups=mesh['grp'=2,'wide'=128,'narrow'=2] {'narrow'}, dimensions={0}, use_global_device_ids=true | all-gather | bytes 1376256 | tf_op jit(solution)/shard_map/all_gather | solution.py:127
  107.4 1.5 %attend.1 = bf16[32,512]{1,0:T(8,128)(2,1)} custom-call(s32[1,128]{1,0:T(1,128)S(1)} %get-tuple-element.7.refs_0_, bf16[96,896]{1,0:T(8,128)(2,1)S(1)} %get-tuple-element.8.refs_1_, bf16[512,896]{1,0:T(8,128)(2,1)S(1)} %all_gather.3.refs_2_), custom_call_target="tpu_custom_call" | custom-call | tf_op jit(solution)/shard_map/attend/pallas_call | solution.py:142
Async XLA Ops:
  2.4 53.9 %copy-start = (bf16[1,1,32,576]{3,2,1,0:T(8,128)(2,1)S(1)}, bf16[1,1,32,576]{3,2,1,0:T(8,128)(2,1)}, u32[]{:S(2)}) copy-start(bf16[1,1,32,576]{3,2,1,0:T(8,128)(2,1)} %param.7) | copy-start | bytes 110596
  2.4 100.4 %all-to-all-start = ((bf16[128,2,896]{2,1,0:T(2,128)(2,1)}), bf16[128,2,896]{2,1,0:T(2,128)(2,1)S(1)}, u32[]{:S(2)}, u32[]{:S(2)}) async-start(bf16[128,2,896]{2,1,0:T(2,128)(2,1)} %pack.1), calls=%async_computation | async-start | bytes 917504 | tf_op jit(solution)/shard_map/all_to_all | solution.py:124
  56.2 0.7 copy-start.1
  56.2 0.7 copy-start.2

commit v3 on v2

--- a/solution.py
+++ b/solution.py
@@ -23,10 +23,38 @@
     return (place % COLUMNS) * rows + row
 
 
-def pack_kernel(rows, slots_ref, cache_ref, packed_ref):
+def pack_kernel(
+    rows,
+    slots_hbm,
+    lengths_hbm,
+    query_hbm,
+    cache_hbm,
+    packed_ref,
+    stacked_ref,
+    limit_ref,
+    slots_ref,
+    lengths_ref,
+    query_ref,
+    cache_ref,
+    arrived,
+):
+    sources = (slots_hbm, cache_hbm, query_hbm, lengths_hbm)
+    places = (slots_ref, cache_ref, query_ref, lengths_ref)
+    copies = [pltpu.make_async_copy(a, b, arrived.at[i]) for i, (a, b) in enumerate(zip(sources, places))]
+    for copy in copies:
+        copy.start()
     count = slots_ref.shape[1]
     rotary = cache_ref.shape[1] - LATENT_WIDTH
     half, half_rotary = LATENT_WIDTH // 2, rotary // 2
+    copies[0].wait()
+    slots = jnp.concatenate([slots_ref[...]] * 2, axis=1)
+    row = lax.broadcasted_iota(jnp.int32, (2 * count, 1), 0)
+    place = row // 2
+    target = partner(place, rows)
+    side = lax.broadcasted_iota(jnp.int32, (1, 2 * count), 1) // count
+    chosen = (slots == target) & (side == row % 2)
+    select = jnp.where(chosen, 1.0, 0.0).astype(cache_ref.dtype)
+    copies[1].wait()
     parts = []
     for h in range(2):
         parts.append(
@@ -42,18 +70,14 @@
             )
         )
     table = jnp.concatenate(parts, axis=1)
-    slots = jnp.concatenate([slots_ref[...]] * 2, axis=1)
-    row = lax.broadcasted_iota(jnp.int32, (2 * count, 1), 0)
-    place = row // 2
-    target = partner(place, rows)
-    side = lax.broadcasted_iota(jnp.int32, (1, 2 * count), 1) // count
-    chosen = (slots == target) & (side == row % 2)
-    select = jnp.where(chosen, 1.0, 0.0).astype(cache_ref.dtype)
     packed = lax.dot_general(select, table, NT, preferred_element_type=jnp.float32).astype(packed_ref.dtype)
     packed_ref[...] = packed.reshape(packed_ref.shape)
-
-
-def query_kernel(me_ref, slots_ref, lengths_ref, query_ref, stacked_ref, limit_ref):
+    copies[2].wait()
+    copies[3].wait()
+    stack_queries(slots_ref, lengths_ref, query_ref, stacked_ref, limit_ref)
+
+
+def stack_queries(slots_ref, lengths_ref, query_ref, stacked_ref, limit_ref):
     heads = query_ref.shape[0]
     rotary = query_ref.shape[1] - LATENT_WIDTH
     half, half_rotary = LATENT_WIDTH // 2, rotary // 2
@@ -67,7 +91,7 @@
         stacked_ref[rows, tail + rotary : tail + rotary + half_rotary] = query_ref[
             :, LATENT_WIDTH + half_rotary * h : LATENT_WIDTH + half_rotary * (h + 1)
         ]
-    own = jnp.where(slots_ref[...] == me_ref[0], lengths_ref[...], 0)
+    own = jnp.where(slots_ref[...] == lax.axis_index("wide"), lengths_ref[...], 0)
     limit_ref[...] = jnp.broadcast_to(1 + jnp.sum(own, axis=1, keepdims=True), limit_ref.shape)
 
 
@@ -115,30 +139,41 @@
     heads = query.shape[2]
     packed_width = LATENT_WIDTH + LATENT_WIDTH // 2 + 2 * rotary
     slot_row = slots.reshape(1, count)
-    packed = pl.pallas_call(
+    vmem = pl.BlockSpec(memory_space=pltpu.VMEM)
+    hbm = pl.BlockSpec(memory_space=pltpu.HBM)
+
+    def held(a):
+        return pltpu.with_memory_space_constraint(a, pltpu.HBM)
+
+    packed, stacked, limit = pl.pallas_call(
         lambda *refs: pack_kernel(rows, *refs),
-        out_shape=jax.ShapeDtypeStruct((count, 2, packed_width), cache.dtype),
+        out_shape=(
+            jax.ShapeDtypeStruct((count, 2, packed_width), cache.dtype),
+            jax.ShapeDtypeStruct((3 * heads, packed_width), query.dtype),
+            jax.ShapeDtypeStruct((1, count), jnp.int32),
+        ),
+        in_specs=[hbm, hbm, hbm, hbm],
+        out_specs=(vmem, vmem, vmem),
+        scratch_shapes=[
+            pltpu.VMEM((1, count), jnp.int32),
+            pltpu.VMEM((1, count), jnp.int32),
+            pltpu.VMEM((heads, channels), query.dtype),
+            pltpu.VMEM((cache.shape[1], channels, count), cache.dtype),
+            pltpu.SemaphoreType.DMA((4,)),
+        ],
+        compiler_params=pltpu.CompilerParams(vmem_limit_bytes=VMEM_BYTES),
         name="pack",
-    )(slot_row, jnp.transpose(cache, (1, 2, 0)))
+    )(
+        held(slot_row),
+        held(lengths.reshape(1, count)),
+        held(query.reshape(heads, channels)),
+        held(jnp.transpose(cache, (1, 2, 0))),
+    )
     order = [partner(place, rows) for place in range(wide_count)]
     received = lax.all_to_all(
         packed, "wide", 0, 0, tiled=True, axis_index_groups=[order]
     )
     keys = lax.all_gather(received.reshape(2 * count, packed_width), "narrow", axis=0, tiled=True)
-    me = lax.axis_index("wide").astype(jnp.int32).reshape(1)
-    vmem = pl.BlockSpec(memory_space=pltpu.VMEM)
-    stacked, limit = pl.pallas_call(
-        query_kernel,
-        out_shape=(
-            jax.ShapeDtypeStruct((3 * heads, packed_width), query.dtype),
-            jax.ShapeDtypeStruct((1, count), jnp.int32),
-        ),
-        in_specs=[pl.BlockSpec(memory_space=pltpu.SMEM), vmem, vmem, vmem],
-        out_specs=(vmem, vmem),
-        compiler_params=pltpu.CompilerParams(vmem_limit_bytes=VMEM_BYTES),
-        cost_estimate=pl.CostEstimate(flops=1 << 22, bytes_accessed=1 << 18, transcendentals=0),
-        name="stack",
-    )(me, slot_row, lengths.reshape(1, count), query.reshape(heads, channels))
     attended = pl.pallas_call(
         lambda *refs: attend_kernel(rows, *refs),
         out_shape=jax.ShapeDtypeStruct((heads, LATENT_WIDTH), jnp.bfloat16),

time: 110 us -> 109 us (level)
  blocking collectives: 4.49 us -> 105 us
  starting transfers between devices: 53.8 us -> 0 us
  waiting for transfers between devices: 45.8 us -> 0 us
    all_to_all x0 -> x1, blocking collectives: none -> 99.8 us  [shards(): lax.all_to_all(packed, 'wide', 0, 0, tiled=True, axis_index_groups=[order])]
    all_to_all x1 -> x0, starting transfers between devices: 53.8 us -> none  [shards(): lax.all_to_all(packed, 'wide', 0, 0, tiled=True, axis_index_groups=[order])]
    all_to_all x1 -> x0, waiting for transfers between devices: 45.8 us -> none  [shards(): lax.all_to_all(packed, 'wide', 0, 0, tiled=True, axis_index_groups=[order])]
    pallas_call x2 -> x1, Pallas kernels: 2.44 us -> 1.51 us  [shards(): pl.pallas_call(lambda *refs: pack_kernel(rows, *refs), out_shape=(jax.Sha...]
  transfers between devices with their start and end apart: 1 -> 0, of which waited for: 1 -> 0; matrix products, arithmetic and copies ran while one was open for 0% -> 0% of each run, Pallas kernels for 0% -> 0%
where the time goes in v3:
time: 109 us; the launch traced here: 108 us
  blocking collectives  105 us (96%)
  Pallas kernels  3.02 us (3%)
    all_to_all x1, blocking collectives, shards(): lax.all_to_all(packed, 'wide', 0, 0, tiled=True, axis_index_groups=[order])  99.8 us
    all_gather x1, blocking collectives, shards(): lax.all_gather(received.reshape(2 * count, packed_width), 'narrow', axis=...  4.78 us

profile of v3, /device:TPU:33, one launch (start us, length us, event | category | flops | bytes accessed | tf_op | source)
XLA Modules:
  0.0 107.7 jit_solution(14435982469878278005)
XLA Ops:
  0.0 1.5 %pack.1 = (bf16[128,2,896]{2,1,0:T(2,128)(2,1)S(1)}, bf16[96,896]{1,0:T(8,128)(2,1)S(1)}, s32[1,128]{1,0:T(1,128)S(1)}) custom-call(s32[1,128]{1,0:T(1,128)} %bitcast.7, s32[1,128]{1,0:T(1,128)} %bitcast.8, bf16[32,576]{1,0:T(8,128)(2,1)} %bitcast.6, bf16[3,576,128]{2,1,0:T(8,128)(2,1)} %bitcast.5), custom_call_target="tpu_custom_call" | custom-call | tf_op jit(solution)/shard_map/pack/pallas_call | solution.py:148
  1.5 99.8 %all_to_all.5 = bf16[128,2,896]{2,1,0:T(2,128)(2,1)S(1)} all-to-all(bf16[128,2,896]{2,1,0:T(2,128)(2,1)S(1)} %get-tuple-element.10), channel_id=1, replica_groups={{0,64,128,192,32,96,160,224,16,80,144,208,48,112,176,240,8,72,136,200,4..., dimensions={0} | all-to-all | bytes 917504 | tf_op jit(solution)/shard_map/all_to_all | solution.py:173
  101.3 0.2 reshape.18
  101.4 4.8 %all_gather.3.refs_2_ = bf16[512,896]{1,0:T(8,128)(2,1)S(1)} all-gather(bf16[256,896]{1,0:T(8,128)(2,1)S(1)} %reshape.18), channel_id=1, replica_groups=mesh['grp'=2,'wide'=128,'narrow'=2] {'narrow'}, dimensions={0}, use_global_device_ids=true | all-gather | bytes 1376256 | tf_op jit(solution)/shard_map/all_gather | solution.py:176
  106.2 1.5 %attend.1 = bf16[32,512]{1,0:T(8,128)(2,1)} custom-call(s32[1,128]{1,0:T(1,128)S(1)} %get-tuple-element.8.refs_0_, bf16[96,896]{1,0:T(8,128)(2,1)S(1)} %get-tuple-element.9.refs_1_, bf16[512,896]{1,0:T(8,128)(2,1)S(1)} %all_gather.3.refs_2_), custom_call_target="tpu_custom_call" | custom-call | tf_op jit(solution)/shard_map/attend/pallas_call | solution.py:177

commit v4 on v3

--- a/solution.py
+++ b/solution.py
@@ -17,9 +17,9 @@
 
 
 def partner(place, rows):
-    step, row = place // COLUMNS, 0
-    for b in range(rows.bit_length() - 1):
-        row = row * 2 + (step >> b) % 2
+    step = place // COLUMNS
+    run = step % 4
+    row = step // 4 + (run % 2) * (rows // 2) + (run // 2) * (rows // 4)
     return (place % COLUMNS) * rows + row
 
 
@@ -97,10 +97,11 @@
 
 def attend_kernel(rows, limit_ref, query_ref, keys_ref, out_ref):
     heads = out_ref.shape[0]
-    width = keys_ref.shape[0]
+    keys = keys_ref[...].reshape(2 * keys_ref.shape[0], keys_ref.shape[2])
+    width = keys.shape[0]
     half = LATENT_WIDTH // 2
     limit = limit_ref[:, :1]
-    scores = lax.dot_general(query_ref[...], keys_ref[...], NT, preferred_element_type=jnp.float32) * score_scale
+    scores = lax.dot_general(query_ref[...], keys, NT, preferred_element_type=jnp.float32) * score_scale
     lane = lax.broadcasted_iota(jnp.int32, (1, width), 1)
     side = lane % 2
     place = (lane // 2) % (width // 4)
@@ -118,11 +119,11 @@
     odd = joined - even
     weight_sum = jnp.sum(whole + even, axis=1, keepdims=True)
     latent = lax.dot_general(
-        whole.astype(keys_ref.dtype), keys_ref[:, :LATENT_WIDTH], NN, preferred_element_type=jnp.float32
+        whole.astype(keys.dtype), keys[:, :LATENT_WIDTH], NN, preferred_element_type=jnp.float32
     )
     halves = lax.dot_general(
-        jnp.concatenate([even, odd], axis=0).astype(keys_ref.dtype),
-        keys_ref[:, LATENT_WIDTH : LATENT_WIDTH + half],
+        jnp.concatenate([even, odd], axis=0).astype(keys.dtype),
+        keys[:, LATENT_WIDTH : LATENT_WIDTH + half],
         NN,
         preferred_element_type=jnp.float32,
     )
@@ -173,7 +174,7 @@
     received = lax.all_to_all(
         packed, "wide", 0, 0, tiled=True, axis_index_groups=[order]
     )
-    keys = lax.all_gather(received.reshape(2 * count, packed_width), "narrow", axis=0, tiled=True)
+    keys = lax.all_gather(received, "narrow", axis=0, tiled=True)
     attended = pl.pallas_call(
         lambda *refs: attend_kernel(rows, *refs),
         out_shape=jax.ShapeDtypeStruct((heads, LATENT_WIDTH), jnp.bfloat16),

time: 109 us -> 109 us (level)
    all_gather x1, blocking collectives: 4.78 us -> 8.01 us  [shards(): keys = lax.all_gather(received, 'narrow', axis=0, tiled=True)]
    all_to_all x1, blocking collectives: 99.8 us -> 96.6 us  [shards(): lax.all_to_all(packed, 'wide', 0, 0, tiled=True, axis_index_groups=[order])]
where the time goes in v4:
time: 109 us; the launch traced here: 108 us
  blocking collectives  105 us (96%)
  Pallas kernels  3.03 us (3%)
    all_to_all x1, blocking collectives, shards(): lax.all_to_all(packed, 'wide', 0, 0, tiled=True, axis_index_groups=[order])  96.6 us
    all_gather x1, blocking collectives, shards(): keys = lax.all_gather(received, 'narrow', axis=0, tiled=True)  8.01 us

profile of v4, /device:TPU:33, one launch (start us, length us, event | category | flops | bytes accessed | tf_op | source)
XLA Modules:
  0.0 107.7 jit_solution(6401938509226932505)
XLA Ops:
  0.0 1.5 %pack.1 = (bf16[128,2,896]{2,1,0:T(2,128)(2,1)S(1)}, bf16[96,896]{1,0:T(8,128)(2,1)S(1)}, s32[1,128]{1,0:T(1,128)S(1)}) custom-call(s32[1,128]{1,0:T(1,128)} %bitcast.7, s32[1,128]{1,0:T(1,128)} %bitcast.8, bf16[32,576]{1,0:T(8,128)(2,1)} %bitcast.6, bf16[3,576,128]{2,1,0:T(8,128)(2,1)} %bitcast.5), custom_call_target="tpu_custom_call" | custom-call | tf_op jit(solution)/shard_map/pack/pallas_call | solution.py:149
  1.5 96.6 %all_to_all.5 = bf16[128,2,896]{2,1,0:T(2,128)(2,1)S(1)} all-to-all(bf16[128,2,896]{2,1,0:T(2,128)(2,1)S(1)} %get-tuple-element.10), channel_id=1, replica_groups={{0,64,128,192,32,96,160,224,16,80,144,208,48,112,176,240,2,66,130,194,3..., dimensions={0} | all-to-all | bytes 917504 | tf_op jit(solution)/shard_map/all_to_all | solution.py:174
  98.1 8.0 %all_gather.3.refs_2_ = bf16[256,2,896]{2,1,0:T(2,128)(2,1)S(1)} all-gather(bf16[128,2,896]{2,1,0:T(2,128)(2,1)S(1)} %all_to_all.5), channel_id=1, replica_groups=mesh['grp'=2,'wide'=128,'narrow'=2] {'narrow'}, dimensions={0}, use_global_device_ids=true | all-gather | bytes 1376256 | tf_op jit(solution)/shard_map/all_gather | solution.py:177
  106.1 1.5 %attend.1 = bf16[32,512]{1,0:T(8,128)(2,1)} custom-call(s32[1,128]{1,0:T(1,128)S(1)} %get-tuple-element.8.refs_0_, bf16[96,896]{1,0:T(8,128)(2,1)S(1)} %get-tuple-element.9.refs_1_, bf16[256,2,896]{2,1,0:T(2,128)(2,1)S(1)} %all_gather.3.refs_2_), custom_call_target="tpu_custom_call" | custom-call | tf_op jit(solution)/shard_map/attend/pallas_call | solution.py:178

commit v5 on v4

--- a/solution.py
+++ b/solution.py
@@ -18,8 +18,9 @@
 
 def partner(place, rows):
     step = place // COLUMNS
-    run = step % 4
-    row = step // 4 + (run % 2) * (rows // 2) + (run // 2) * (rows // 4)
+    run, turn = step % 4, step // 4
+    row = turn + (run % 2) * (rows // 2) + (run // 2) * (rows // 4)
+    row = row + (run // 3) * (rows // 4 - 1 - 2 * turn)
     return (place % COLUMNS) * rows + row
 
 
@@ -38,8 +39,8 @@
     cache_ref,
     arrived,
 ):
-    sources = (slots_hbm, cache_hbm, query_hbm, lengths_hbm)
-    places = (slots_ref, cache_ref, query_ref, lengths_ref)
+    sources = (slots_hbm, query_hbm, lengths_hbm, cache_hbm)
+    places = (slots_ref, query_ref, lengths_ref, cache_ref)
     copies = [pltpu.make_async_copy(a, b, arrived.at[i]) for i, (a, b) in enumerate(zip(sources, places))]
     for copy in copies:
         copy.start()
@@ -55,6 +56,9 @@
     chosen = (slots == target) & (side == row % 2)
     select = jnp.where(chosen, 1.0, 0.0).astype(cache_ref.dtype)
     copies[1].wait()
+    copies[2].wait()
+    stack_queries(slots_ref, lengths_ref, query_ref, stacked_ref, limit_ref)
+    copies[3].wait()
     parts = []
     for h in range(2):
         parts.append(
@@ -72,9 +76,6 @@
     table = jnp.concatenate(parts, axis=1)
     packed = lax.dot_general(select, table, NT, preferred_element_type=jnp.float32).astype(packed_ref.dtype)
     packed_ref[...] = packed.reshape(packed_ref.shape)
-    copies[2].wait()
-    copies[3].wait()
-    stack_queries(slots_ref, lengths_ref, query_ref, stacked_ref, limit_ref)
 
 
 def stack_queries(slots_ref, lengths_ref, query_ref, stacked_ref, limit_ref):

time: 109 us -> 108 us (level); the launches traced: 108 us -> 108 us
  no operation moved by 1% of the time
where the time goes in v5:
time: 108 us
  blocking collectives  105 us (97%)
  Pallas kernels  2.99 us (3%)
    all_to_all x1, blocking collectives, shards(): lax.all_to_all(packed, 'wide', 0, 0, tiled=True, axis_index_groups=[order])  96.3 us
    all_gather x1, blocking collectives, shards(): keys = lax.all_gather(received, 'narrow', axis=0, tiled=True)  8.74 us

profile of v5, /device:TPU:33, one launch (start us, length us, event | category | flops | bytes accessed | tf_op | source)
XLA Modules:
  0.0 108.0 jit_solution(7338586420609576336)
XLA Ops:
  0.0 1.5 %pack.1 = (bf16[128,2,896]{2,1,0:T(2,128)(2,1)S(1)}, bf16[96,896]{1,0:T(8,128)(2,1)S(1)}, s32[1,128]{1,0:T(1,128)S(1)}) custom-call(s32[1,128]{1,0:T(1,128)} %bitcast.7, s32[1,128]{1,0:T(1,128)} %bitcast.8, bf16[32,576]{1,0:T(8,128)(2,1)} %bitcast.6, bf16[3,576,128]{2,1,0:T(8,128)(2,1)} %bitcast.5), custom_call_target="tpu_custom_call" | custom-call | tf_op jit(solution)/shard_map/pack/pallas_call | solution.py:150
  1.5 96.3 %all_to_all.5 = bf16[128,2,896]{2,1,0:T(2,128)(2,1)S(1)} all-to-all(bf16[128,2,896]{2,1,0:T(2,128)(2,1)S(1)} %get-tuple-element.10), channel_id=1, replica_groups={{0,64,128,192,32,96,160,224,16,80,144,208,62,126,190,254,2,66,130,194,3..., dimensions={0} | all-to-all | bytes 917504 | tf_op jit(solution)/shard_map/all_to_all | solution.py:175
  97.8 8.7 %all_gather.3.refs_2_ = bf16[256,2,896]{2,1,0:T(2,128)(2,1)S(1)} all-gather(bf16[128,2,896]{2,1,0:T(2,128)(2,1)S(1)} %all_to_all.5), channel_id=1, replica_groups=mesh['grp'=2,'wide'=128,'narrow'=2] {'narrow'}, dimensions={0}, use_global_device_ids=true | all-gather | bytes 1376256 | tf_op jit(solution)/shard_map/all_gather | solution.py:178
  106.5 1.5 %attend.1 = bf16[32,512]{1,0:T(8,128)(2,1)} custom-call(s32[1,128]{1,0:T(1,128)S(1)} %get-tuple-element.8.refs_0_, bf16[96,896]{1,0:T(8,128)(2,1)S(1)} %get-tuple-element.9.refs_1_, bf16[256,2,896]{2,1,0:T(2,128)(2,1)S(1)} %all_gather.3.refs_2_), custom_call_target="tpu_custom_call" | custom-call | tf_op jit(solution)/shard_map/attend/pallas_call | solution.py:179

commit v6 on v5

--- a/solution.py
+++ b/solution.py
@@ -22,6 +22,14 @@
     row = turn + (run % 2) * (rows // 2) + (run // 2) * (rows // 4)
     row = row + (run // 3) * (rows // 4 - 1 - 2 * turn)
     return (place % COLUMNS) * rows + row
+
+
+def place_of(wide, rows):
+    column, row = wide // rows, wide % rows
+    quarter, turn = row // (rows // 4), row % (rows // 4)
+    run = quarter % 2 * 2 + quarter // 2
+    turn = turn + (quarter // 3) * (rows // 4 - 1 - 2 * turn)
+    return (turn * 4 + run) * COLUMNS + column
 
 
 def pack_kernel(
@@ -48,12 +56,9 @@
     rotary = cache_ref.shape[1] - LATENT_WIDTH
     half, half_rotary = LATENT_WIDTH // 2, rotary // 2
     copies[0].wait()
-    slots = jnp.concatenate([slots_ref[...]] * 2, axis=1)
-    row = lax.broadcasted_iota(jnp.int32, (2 * count, 1), 0)
-    place = row // 2
-    target = partner(place, rows)
-    side = lax.broadcasted_iota(jnp.int32, (1, 2 * count), 1) // count
-    chosen = (slots == target) & (side == row % 2)
+    places_of = place_of(slots_ref[...], rows)
+    lane_key = jnp.concatenate([2 * places_of, 2 * places_of + 1], axis=1)
+    chosen = lane_key == lax.broadcasted_iota(jnp.int32, (2 * count, 2 * count), 0)
     select = jnp.where(chosen, 1.0, 0.0).astype(cache_ref.dtype)
     copies[1].wait()
     copies[2].wait()
@@ -82,16 +87,22 @@
     heads = query_ref.shape[0]
     rotary = query_ref.shape[1] - LATENT_WIDTH
     half, half_rotary = LATENT_WIDTH // 2, rotary // 2
-    stacked_ref[...] = jnp.zeros_like(stacked_ref)
-    tail = LATENT_WIDTH + half
-    stacked_ref[:heads, :LATENT_WIDTH] = query_ref[:, :LATENT_WIDTH]
-    stacked_ref[:heads, tail : tail + rotary] = query_ref[:, LATENT_WIDTH:]
+    latent = query_ref[:, :LATENT_WIDTH]
+    turned = query_ref[:, LATENT_WIDTH:].astype(jnp.float32)
+    turned = jnp.concatenate([turned, jnp.zeros_like(turned)], axis=1)
+    lane = lax.broadcasted_iota(jnp.int32, (1, 2 * rotary), 1)
+    shared = (lane >= rotary) & (lane < rotary + half_rotary)
+
+    def blank(n):
+        return jnp.zeros((heads, n), latent.dtype)
+
+    stacked_ref[:heads] = jnp.concatenate([latent, blank(half), turned.astype(latent.dtype)], axis=1)
     for h in range(2):
-        rows = pl.ds(heads * (h + 1), heads)
-        stacked_ref[rows, LATENT_WIDTH:tail] = query_ref[:, half * h : half * (h + 1)]
-        stacked_ref[rows, tail + rotary : tail + rotary + half_rotary] = query_ref[
-            :, LATENT_WIDTH + half_rotary * h : LATENT_WIDTH + half_rotary * (h + 1)
-        ]
+        moved = jnp.where(shared, pltpu.roll(turned, rotary - half_rotary * h, 1), 0.0)
+        part = latent[:, half * h : half * (h + 1)]
+        stacked_ref[heads * (h + 1) : heads * (h + 2)] = jnp.concatenate(
+            [blank(LATENT_WIDTH), part, moved.astype(latent.dtype)], axis=1
+        )
     own = jnp.where(slots_ref[...] == lax.axis_index("wide"), lengths_ref[...], 0)
     limit_ref[...] = jnp.broadcast_to(1 + jnp.sum(own, axis=1, keepdims=True), limit_ref.shape)
 

time: 108 us -> 108 us (level)
  no operation moved by 1% of the time
where the time goes in v6:
time: 108 us
  blocking collectives  105 us (97%)
  Pallas kernels  2.97 us (3%)
    all_to_all x1, blocking collectives, shards(): lax.all_to_all(packed, 'wide', 0, 0, tiled=True, axis_index_groups=[order])  96.3 us
    all_gather x1, blocking collectives, shards(): keys = lax.all_gather(received, 'narrow', axis=0, tiled=True)  8.74 us

profile of v6, /device:TPU:33, one launch (start us, length us, event | category | flops | bytes accessed | tf_op | source)
XLA Modules:
  0.0 108.0 jit_solution(10001937241559254803)
XLA Ops:
  0.0 1.4 %pack.1 = (bf16[128,2,896]{2,1,0:T(2,128)(2,1)S(1)}, bf16[96,896]{1,0:T(8,128)(2,1)S(1)}, s32[1,128]{1,0:T(1,128)S(1)}) custom-call(s32[1,128]{1,0:T(1,128)} %bitcast.7, s32[1,128]{1,0:T(1,128)} %bitcast.8, bf16[32,576]{1,0:T(8,128)(2,1)} %bitcast.6, bf16[3,576,128]{2,1,0:T(8,128)(2,1)} %bitcast.5), custom_call_target="tpu_custom_call" | custom-call | tf_op jit(solution)/shard_map/pack/pallas_call | solution.py:161
  1.5 96.3 %all_to_all.5 = bf16[128,2,896]{2,1,0:T(2,128)(2,1)S(1)} all-to-all(bf16[128,2,896]{2,1,0:T(2,128)(2,1)S(1)} %get-tuple-element.10), channel_id=1, replica_groups={{0,64,128,192,32,96,160,224,16,80,144,208,62,126,190,254,2,66,130,194,3..., dimensions={0} | all-to-all | bytes 917504 | tf_op jit(solution)/shard_map/all_to_all | solution.py:186
  97.8 8.7 %all_gather.3.refs_2_ = bf16[256,2,896]{2,1,0:T(2,128)(2,1)S(1)} all-gather(bf16[128,2,896]{2,1,0:T(2,128)(2,1)S(1)} %all_to_all.5), channel_id=1, replica_groups=mesh['grp'=2,'wide'=128,'narrow'=2] {'narrow'}, dimensions={0}, use_global_device_ids=true | all-gather | bytes 1376256 | tf_op jit(solution)/shard_map/all_gather | solution.py:189
  106.5 1.5 %attend.1 = bf16[32,512]{1,0:T(8,128)(2,1)} custom-call(s32[1,128]{1,0:T(1,128)S(1)} %get-tuple-element.8.refs_0_, bf16[96,896]{1,0:T(8,128)(2,1)S(1)} %get-tuple-element.9.refs_1_, bf16[256,2,896]{2,1,0:T(2,128)(2,1)S(1)} %all_gather.3.refs_2_), custom_call_target="tpu_custom_call" | custom-call | tf_op jit(solution)/shard_map/attend/pallas_call | solution.py:190

commit v7 on v6

--- a/solution.py
+++ b/solution.py
@@ -40,7 +40,7 @@
     cache_hbm,
     packed_ref,
     stacked_ref,
-    limit_ref,
+    visible_ref,
     slots_ref,
     lengths_ref,
     query_ref,
@@ -62,7 +62,7 @@
     select = jnp.where(chosen, 1.0, 0.0).astype(cache_ref.dtype)
     copies[1].wait()
     copies[2].wait()
-    stack_queries(slots_ref, lengths_ref, query_ref, stacked_ref, limit_ref)
+    stack_queries(rows, slots_ref, lengths_ref, query_ref, stacked_ref, visible_ref)
     copies[3].wait()
     parts = []
     for h in range(2):
@@ -83,7 +83,7 @@
     packed_ref[...] = packed.reshape(packed_ref.shape)
 
 
-def stack_queries(slots_ref, lengths_ref, query_ref, stacked_ref, limit_ref):
+def stack_queries(wide_rows, slots_ref, lengths_ref, query_ref, stacked_ref, visible_ref):
     heads = query_ref.shape[0]
     rotary = query_ref.shape[1] - LATENT_WIDTH
     half, half_rotary = LATENT_WIDTH // 2, rotary // 2
@@ -104,26 +104,29 @@
             [blank(LATENT_WIDTH), part, moved.astype(latent.dtype)], axis=1
         )
     own = jnp.where(slots_ref[...] == lax.axis_index("wide"), lengths_ref[...], 0)
-    limit_ref[...] = jnp.broadcast_to(1 + jnp.sum(own, axis=1, keepdims=True), limit_ref.shape)
-
-
-def attend_kernel(rows, limit_ref, query_ref, keys_ref, out_ref):
+    limit = 1 + jnp.sum(own, axis=1, keepdims=True)
+    width = visible_ref.shape[1]
+    lane = lax.broadcasted_iota(jnp.int32, (1, width), 1)
+    side = lane % 2
+    source = partner((lane // 2) % (width // 4), wide_rows)
+    first = (source * 2 + lane // (width // 2)) * 3
+    visible_ref[:1] = (first + side < limit).astype(jnp.int32)
+    visible_ref[1:] = (first + 2 < limit).astype(jnp.int32)
+
+
+def attend_kernel(visible_ref, query_ref, keys_ref, out_ref):
     heads = out_ref.shape[0]
     keys = keys_ref[...].reshape(2 * keys_ref.shape[0], keys_ref.shape[2])
     width = keys.shape[0]
     half = LATENT_WIDTH // 2
-    limit = limit_ref[:, :1]
     scores = lax.dot_general(query_ref[...], keys, NT, preferred_element_type=jnp.float32) * score_scale
     lane = lax.broadcasted_iota(jnp.int32, (1, width), 1)
     side = lane % 2
-    place = (lane // 2) % (width // 4)
-    source = partner(place, rows)
-    first = (source * 2 + lane // (width // 2)) * 3
     whole = scores[:heads]
     part = jnp.where(side == 0, scores[heads : 2 * heads], scores[2 * heads :])
     joined = part + jnp.where(side == 0, pltpu.roll(part, width - 1, 1), pltpu.roll(part, 1, 1))
-    whole = jnp.where(first + side < limit, whole, floor_value)
-    joined = jnp.where(first + 2 < limit, joined, floor_value)
+    whole = jnp.where(visible_ref[:1] > 0, whole, floor_value)
+    joined = jnp.where(visible_ref[1:] > 0, joined, floor_value)
     highest = jnp.max(jnp.maximum(whole, joined), axis=1, keepdims=True)
     whole = jnp.exp(whole - highest)
     joined = jnp.exp(joined - highest)
@@ -158,12 +161,12 @@
     def held(a):
         return pltpu.with_memory_space_constraint(a, pltpu.HBM)
 
-    packed, stacked, limit = pl.pallas_call(
+    packed, stacked, visible = pl.pallas_call(
         lambda *refs: pack_kernel(rows, *refs),
         out_shape=(
             jax.ShapeDtypeStruct((count, 2, packed_width), cache.dtype),
             jax.ShapeDtypeStruct((3 * heads, packed_width), query.dtype),
-            jax.ShapeDtypeStruct((1, count), jnp.int32),
+            jax.ShapeDtypeStruct((2, 4 * count), jnp.int32),
         ),
         in_specs=[hbm, hbm, hbm, hbm],
         out_specs=(vmem, vmem, vmem),
@@ -188,13 +191,13 @@
     )
     keys = lax.all_gather(received, "narrow", axis=0, tiled=True)
     attended = pl.pallas_call(
-        lambda *refs: attend_kernel(rows, *refs),
+        attend_kernel,
         out_shape=jax.ShapeDtypeStruct((heads, LATENT_WIDTH), jnp.bfloat16),
         in_specs=[vmem, vmem, vmem],
         out_specs=vmem,
         compiler_params=pltpu.CompilerParams(vmem_limit_bytes=VMEM_BYTES),
         name="attend",
-    )(limit, stacked, keys)
+    )(visible, stacked, keys)
     return attended.reshape(1, 1, heads, LATENT_WIDTH)
 
 

time: 108 us -> 108 us (level)
  no operation moved by 1% of the time
where the time goes in v7:
time: 108 us
  blocking collectives  105 us (97%)
  Pallas kernels  2.97 us (3%)
    all_to_all x1, blocking collectives, shards(): lax.all_to_all(packed, 'wide', 0, 0, tiled=True, axis_index_groups=[order])  96.3 us
    all_gather x1, blocking collectives, shards(): keys = lax.all_gather(received, 'narrow', axis=0, tiled=True)  8.74 us

profile of v7, /device:TPU:33, one launch (start us, length us, event | category | flops | bytes accessed | tf_op | source)
XLA Modules:
  0.0 108.0 jit_solution(11949846142857324318)
XLA Ops:
  0.0 1.4 %pack.1 = (bf16[128,2,896]{2,1,0:T(2,128)(2,1)S(1)}, bf16[96,896]{1,0:T(8,128)(2,1)S(1)}, s32[2,512]{1,0:T(2,128)S(1)}) custom-call(s32[1,128]{1,0:T(1,128)} %bitcast.7, s32[1,128]{1,0:T(1,128)} %bitcast.8, bf16[32,576]{1,0:T(8,128)(2,1)} %bitcast.6, bf16[3,576,128]{2,1,0:T(8,128)(2,1)} %bitcast.5), custom_call_target="tpu_custom_call" | custom-call | tf_op jit(solution)/shard_map/pack/pallas_call | solution.py:164
  1.5 96.3 %all_to_all.5 = bf16[128,2,896]{2,1,0:T(2,128)(2,1)S(1)} all-to-all(bf16[128,2,896]{2,1,0:T(2,128)(2,1)S(1)} %get-tuple-element.10), channel_id=1, replica_groups={{0,64,128,192,32,96,160,224,16,80,144,208,62,126,190,254,2,66,130,194,3..., dimensions={0} | all-to-all | bytes 917504 | tf_op jit(solution)/shard_map/all_to_all | solution.py:189
  97.8 8.7 %all_gather.3.keys_ref = bf16[256,2,896]{2,1,0:T(2,128)(2,1)S(1)} all-gather(bf16[128,2,896]{2,1,0:T(2,128)(2,1)S(1)} %all_to_all.5), channel_id=1, replica_groups=mesh['grp'=2,'wide'=128,'narrow'=2] {'narrow'}, dimensions={0}, use_global_device_ids=true | all-gather | bytes 1376256 | tf_op jit(solution)/shard_map/all_gather | solution.py:192
  106.5 1.5 %attend.1 = bf16[32,512]{1,0:T(8,128)(2,1)} custom-call(s32[2,512]{1,0:T(2,128)S(1)} %get-tuple-element.8.visible_ref, bf16[96,896]{1,0:T(8,128)(2,1)S(1)} %get-tuple-element.9.query_ref, bf16[256,2,896]{2,1,0:T(2,128)(2,1)S(1)} %all_gather.3.keys_ref), custom_call_target="tpu_custom_call" | custom-call | tf_op jit(solution)/shard_map/attend/pallas_call | solution.py:193

commit v8 on v6

--- a/solution.py
+++ b/solution.py
@@ -140,7 +140,7 @@
         preferred_element_type=jnp.float32,
     )
     latent = latent + jnp.concatenate([halves[:heads], halves[heads:]], axis=1)
-    out_ref[...] = (latent / weight_sum).astype(out_ref.dtype)
+    out_ref[...] = (latent * (1.0 / weight_sum)).astype(out_ref.dtype)
 
 
 def shards(cache, lengths, slots, query):

time: 108 us -> 108 us (level)
  no operation moved by 1% of the time
where the time goes in v8:
time: 108 us
  blocking collectives  105 us (97%)
  Pallas kernels  2.97 us (3%)
    all_to_all x1, blocking collectives, shards(): lax.all_to_all(packed, 'wide', 0, 0, tiled=True, axis_index_groups=[order])  96.3 us
    all_gather x1, blocking collectives, shards(): keys = lax.all_gather(received, 'narrow', axis=0, tiled=True)  8.74 us

profile of v8, /device:TPU:33, one launch (start us, length us, event | category | flops | bytes accessed | tf_op | source)
XLA Modules:
  0.0 108.0 jit_solution(10001937241559254803)
XLA Ops:
  0.0 1.4 %pack.1 = (bf16[128,2,896]{2,1,0:T(2,128)(2,1)S(1)}, bf16[96,896]{1,0:T(8,128)(2,1)S(1)}, s32[1,128]{1,0:T(1,128)S(1)}) custom-call(s32[1,128]{1,0:T(1,128)} %bitcast.7, s32[1,128]{1,0:T(1,128)} %bitcast.8, bf16[32,576]{1,0:T(8,128)(2,1)} %bitcast.6, bf16[3,576,128]{2,1,0:T(8,128)(2,1)} %bitcast.5), custom_call_target="tpu_custom_call" | custom-call | tf_op jit(solution)/shard_map/pack/pallas_call | solution.py:161
  1.5 96.3 %all_to_all.5 = bf16[128,2,896]{2,1,0:T(2,128)(2,1)S(1)} all-to-all(bf16[128,2,896]{2,1,0:T(2,128)(2,1)S(1)} %get-tuple-element.10), channel_id=1, replica_groups={{0,64,128,192,32,96,160,224,16,80,144,208,62,126,190,254,2,66,130,194,3..., dimensions={0} | all-to-all | bytes 917504 | tf_op jit(solution)/shard_map/all_to_all | solution.py:186
  97.8 8.7 %all_gather.3.refs_2_ = bf16[256,2,896]{2,1,0:T(2,128)(2,1)S(1)} all-gather(bf16[128,2,896]{2,1,0:T(2,128)(2,1)S(1)} %all_to_all.5), channel_id=1, replica_groups=mesh['grp'=2,'wide'=128,'narrow'=2] {'narrow'}, dimensions={0}, use_global_device_ids=true | all-gather | bytes 1376256 | tf_op jit(solution)/shard_map/all_gather | solution.py:189
  106.5 1.5 %attend.1 = bf16[32,512]{1,0:T(8,128)(2,1)} custom-call(s32[1,128]{1,0:T(1,128)S(1)} %get-tuple-element.8.refs_0_, bf16[96,896]{1,0:T(8,128)(2,1)S(1)} %get-tuple-element.9.refs_1_, bf16[256,2,896]{2,1,0:T(2,128)(2,1)S(1)} %all_gather.3.refs_2_), custom_call_target="tpu_custom_call" | custom-call | tf_op jit(solution)/shard_map/attend/pallas_call | solution.py:190
